TPU v7x, 32 devices: a whole 2x2x4 slice. The times are simulated.
32 devices in a mesh: param: 16 (over z, y, x), sensor: 2 (over core).
Axes of the slice: x: 2, y: 2, z: 4, core: 2. Of those that a mesh axis runs over, the one named last changes fastest.
Arguments:
- data: float32 [16, 512, 420], P(None, ('sensor', 'param')), may hold values from -6 to 6
- spectra: float32 [2, 512, 64, 421], P(None, 'sensor', 'param'), may hold values from -2 to 2
Outputs:
- gradient: float32 [16, 64, 420], P(None, 'param')
- rms: float32 [16], replicated
All inputs are finite; a program needn't handle non-finite values.
Results may differ from a plain program's by a relative error of at most 0.0003.
Values sent between devices are 32-bit elements; how exact they have to be, the bound alone decides.
A program may use at most 128 MiB of HBM per device.

v0:
```python
import math

import jax
import jax.numpy as jnp
from jax import lax
from jax.sharding import PartitionSpec as P


def spectral_tables(steps):
    length = 2 * steps
    freqs = steps + 1
    times = lax.broadcasted_iota(jnp.int32, (steps, freqs), 0)
    bins = lax.broadcasted_iota(jnp.int32, (steps, freqs), 1)
    phase = 2.0 * math.pi / length * (times * bins % length).astype(jnp.float32)
    forward = jnp.concatenate([jnp.cos(phase), -jnp.sin(phase)], axis=1)
    weight = jnp.where((bins == 0) | (bins == steps), 1.0, 2.0) / length
    backward = jnp.concatenate([(weight * jnp.cos(phase)).T, (-weight * jnp.sin(phase)).T], axis=0)
    return (forward, backward)


def to_spectrum(series, forward):
    vectors, sensors, steps = series.shape
    flat = jnp.dot(
        series.reshape(vectors * sensors, steps),
        forward,
        precision=lax.Precision.HIGHEST,
        preferred_element_type=jnp.float32,
    )
    return flat.reshape(vectors, sensors, forward.shape[1])


def contract(kernel, spectrum):
    return jnp.einsum(
        "spf,rsf->rpf",
        kernel,
        spectrum,
        precision=lax.Precision.HIGHEST,
        preferred_element_type=jnp.float32,
    )


def body(data, spectra):
    steps = data.shape[2]
    freqs = steps + 1
    forward, backward = spectral_tables(steps)
    whole = to_spectrum(lax.all_gather(data, "param", axis=1, tiled=True), forward)
    real_part = whole[..., :freqs]
    imag_part = whole[..., freqs:]
    kernel_re = spectra[0]
    kernel_im = spectra[1]
    out_re = contract(kernel_re, real_part) + contract(kernel_im, imag_part)
    out_im = contract(kernel_re, imag_part) - contract(kernel_im, real_part)
    vectors, points = (out_re.shape[0], out_re.shape[1])
    stacked = jnp.concatenate([out_re, out_im], axis=2).reshape(vectors * points, 2 * freqs)
    partial_field = jnp.dot(
        stacked, backward, precision=lax.Precision.HIGHEST, preferred_element_type=jnp.float32
    ).reshape(vectors, points, steps)
    count = points * lax.axis_size("param") * steps
    share = lax.psum_scatter(partial_field, "sensor", scatter_dimension=0, tiled=True)
    squares = lax.psum(jnp.sum(share * share, axis=(1, 2)), "param")
    scale = jnp.sqrt(squares / count + 1e-06)
    normalized = share / scale[:, None, None]
    gradient, rms_all = (
        lax.all_gather(normalized, "sensor", axis=0, tiled=True),
        lax.all_gather(scale, "sensor", axis=0, tiled=True),
    )
    return (gradient, rms_all)


def solution(mesh):
    in_specs = (P(None, ("sensor", "param"), None), P(None, "sensor", "param", None))
    out_specs = (P(None, "param", None), P())
    return jax.shard_map(body, mesh=mesh, in_specs=in_specs, out_specs=out_specs, check_vma=False)
```

profile of v0, /device:TPU:1, one launch (start us, length us, event | category | flops | bytes accessed | tf_op | source)
XLA Modules:
  0.0 326.4 jit_solution(8645191133042081712)
XLA Ops:
  7.2 0.0 all-gather.2.cloned.1.call-start
  7.2 0.7 all-gather.2.cloned.1.call-update
  7.9 0.0 reduce-scatter.2.cloned.1.call-start
  8.0 4.5 %sine_negate_fusion = (f32[420,421]{1,0:T(8,128)}, f32[420,421]{1,0:T(8,128)}) fusion(), kind=kLoop, calls=%fused_computation.39 | loop fusion | flops 1768200 | bytes 1414560 | tf_op jit(solution)/shard_map/neg | solution.py:15
  12.5 4.6 %sine_multiply_fusion = (f32[421,420]{0,1:T(8,128)}, f32[421,420]{0,1:T(8,128)}) fusion(f32[421]{0:T(512)S(1)} %fusion.42, f32[421]{0:T(512)S(1)} %select_multiply_fusion), kind=kLoop, calls=%fused_computation.34 | loop fusion | flops 1945020 | bytes 1417928 | tf_op jit(solution)/shard_map/mul | solution.py:17
  17.0 1.5 fusion.73
  18.5 1.5 fusion.71
  20.0 1.5 fusion.75
  21.6 1.5 fusion.77
  23.1 100.8 %all-gather.2.cloned.1.call-done = f32[16,256,420]{2,1,0:T(8,128)} async-done(((f32[16,16,420]{2,1,0:T(8,128)}), f32[16,256,420]{2,1,0:T(8,128)}) %all-gather.2.cloned.1.call-update) | async-done | bytes 6881296 | tf_op jit(solution)/shard_map/all_gather | solution.py:46
  123.9 51.7 %fusion.20 = f32[842,4096]{1,0:T(8,128)} fusion(f32[4096,420]{1,0:T(8,128)} %bitcast.71, f32[420,421]{1,0:T(8,128)} %get-tuple-element.6, f32[420,421]{1,0:T(8,128)} %get-tuple-element.7), kind=kOutput, calls=%fused_computation.20 | convolution fusion | flops 17382467584 | bytes 22091168 | tf_op jit(solution)/shard_map/dot_general | solution.py:23
  175.6 16.8 %copy.9 = f32[106,8,16,256]{3,2,1,0:T(8,128)} copy(f32[106,8,16,256]{3,1,2,0:T(8,128)} %bitcast.70) | data formatting | bytes 27787264
  192.4 14.2 %fusion.2 = f32[421,16,4]{1,2,0:T(4,128)} fusion(f32[848,16,256]{2,1,0:T(8,128)} %bitcast.66, f32[256,4,421]{0,1,2:T(4,128)S(1)} %copy-done.4), kind=kOutput, calls=%fused_computation.2 | convolution fusion | flops 82771968 | bytes 15627520 | tf_op jit(solution)/shard_map/spf,rsf->rpf/dot_general | solution.py:33
  206.6 2.1 copy.5
  208.7 14.2 %fusion = f32[421,16,4]{1,2,0:T(4,128)} fusion(f32[848,16,256]{2,1,0:T(8,128)} %bitcast.67, f32[256,4,421]{0,1,2:T(4,128)S(1)} %copy-done.3), kind=kOutput, calls=%fused_computation | convolution fusion | flops 82771968 | bytes 15627520 | tf_op jit(solution)/shard_map/spf,rsf->rpf/dot_general | solution.py:33
  222.9 2.1 copy.6
  225.0 14.3 %fusion.4 = f32[421,16,4]{1,2,0:T(4,128)} fusion(f32[848,16,256]{2,1,0:T(8,128)} %bitcast.68, f32[256,4,421]{0,1,2:T(4,128)S(1)} %copy-done.2), kind=kOutput, calls=%fused_computation.4 | convolution fusion | flops 82771968 | bytes 15627520 | tf_op jit(solution)/shard_map/spf,rsf->rpf/dot_general | solution.py:33
  239.3 2.1 copy.7
  241.4 14.1 %fusion.6 = f32[421,16,4]{1,2,0:T(4,128)} fusion(f32[848,16,256]{2,1,0:T(8,128)} %bitcast.69, f32[256,4,421]{0,1,2:T(4,128)S(1)} %copy-done.1), kind=kOutput, calls=%fused_computation.6 | convolution fusion | flops 82771968 | bytes 15627520 | tf_op jit(solution)/shard_map/spf,rsf->rpf/dot_general | solution.py:33
  255.5 1.5 copy.8
  257.0 1.0 add_bitcast_fusion
  258.0 0.9 subtract_bitcast_fusion
  258.9 2.3 fusion.24
  261.2 0.6 dynamic-slice
  261.8 7.3 %reduce-scatter.2.cloned.1.call-done = f32[8,4,420]{2,0,1:T(8,128)} async-done(((f32[16,4,420]{2,0,1:T(8,128)}), f32[8,4,420]{2,0,1:T(8,128)}) %reduce-scatter.2.cloned.1.call-update) | async-done | bytes 53776 | tf_op jit(solution)/shard_map/reduce_scatter | solution.py:59
  269.2 1.0 multiply_reduce_fusion
  270.8 35.2 %psum.7 = f32[8]{0:T(128)S(1)} all-reduce(f32[8]{0:T(128)S(1)} %multiply_reduce_fusion), channel_id=1, replica_groups=mesh['param'=16,'sensor'=2] {'param'}, use_global_device_ids=true, to_apply=%region_2.3 | all-reduce | flops 8 | bytes 64 | tf_op jit(solution)/shard_map/psum | solution.py:60
  306.0 0.1 fusion.45
  306.1 0.9 broadcast_divide_fusion
  307.0 8.6 %all_gather.10 = f32[16,4,420]{2,0,1:T(8,128)S(1)} all-gather(f32[8,4,420]{2,0,1:T(8,128)S(1)} %broadcast_divide_fusion), channel_id=1, replica_groups=mesh['param'=16,'sensor'=2] {'sensor'}, dimensions={0}, use_global_device_ids=true | all-gather | bytes 161280 | tf_op jit(solution)/shard_map/all_gather | solution.py:64
  315.6 0.7 copy.4
  316.3 3.0 all-reduce
  (20 shorter events, 0.1 us)
Async XLA Ops:
  7.2 9.9 %copy-start = (f32[2,256,4,421]{1,2,3,0:T(4,128)S(1)}, f32[2,256,4,421]{1,2,3,0:T(4,128)}, u32[]{:S(2)}) copy-start(f32[2,256,4,421]{1,2,3,0:T(4,128)} %param.3) | copy-start | bytes 10346500
  7.2 116.7 %all-gather.2.cloned.1.call-start = ((), (), s32[]{:S(2)}) async-start(), calls=%async_computation.1 | async-start | bytes 8912896 | tf_op jit(solution)/shard_map/all_gather | solution.py:46
  7.9 261.3 %reduce-scatter.2.cloned.1.call-start = ((), (), s32[]{:S(2)}) async-start(), calls=%async_computation.2 | async-start | bytes 196608 | tf_op jit(solution)/shard_map/reduce_scatter | solution.py:59
  175.5 16.8 %copy-start.4 = (f32[256,4,421]{0,1,2:T(4,128)S(1)}, f32[256,4,421]{0,1,2:T(4,128)}, u32[]{:S(2)}) copy-start(f32[256,4,421]{0,1,2:T(4,128)} %fusion.73) | copy-start | bytes 5173252
  192.4 16.3 %copy-start.3 = (f32[256,4,421]{0,1,2:T(4,128)S(1)}, f32[256,4,421]{0,1,2:T(4,128)}, u32[]{:S(2)}) copy-start(f32[256,4,421]{0,1,2:T(4,128)} %fusion.71) | copy-start | bytes 5173252
  208.7 16.3 %copy-start.2 = (f32[256,4,421]{0,1,2:T(4,128)S(1)}, f32[256,4,421]{0,1,2:T(4,128)}, u32[]{:S(2)}) copy-start(f32[256,4,421]{0,1,2:T(4,128)} %fusion.75) | copy-start | bytes 5173252
  225.0 16.4 %copy-start.1 = (f32[256,4,421]{0,1,2:T(4,128)S(1)}, f32[256,4,421]{0,1,2:T(4,128)}, u32[]{:S(2)}) copy-start(f32[256,4,421]{0,1,2:T(4,128)} %fusion.77) | copy-start | bytes 5173252
  241.4 17.5 %copy-start.5 = (f32[421,420]{0,1:T(8,128)S(1)}, f32[421,420]{0,1:T(8,128)}, u32[]{:S(2)}) copy-start(f32[421,420]{0,1:T(8,128)} %get-tuple-element.8) | copy-start | bytes 2121844
  241.4 17.5 %copy-start.6 = (f32[421,420]{0,1:T(8,128)S(1)}, f32[421,420]{0,1:T(8,128)}, u32[]{:S(2)}) copy-start(f32[421,420]{0,1:T(8,128)} %get-tuple-element.9) | copy-start | bytes 2121844
  255.5 5.7 %copy-start.7 = (u32[32]{0:T(128)S(1)}, u32[32]{0:T(128)}, u32[]{:S(2)}) copy-start(u32[32]{0:T(128)} %constant.35) | copy-start | bytes 388
Sparse Core Ops, SparseCore 0:
  10.8 113.0 all-gather.1
  261.4 7.7 reduce-scatter.1
where the time goes:
time: 330 us; the launch traced here: 326 us
  matrix products  111 us (34%)
  waiting for transfers between devices  109 us (33%)
  blocking collectives  46.7 us (14%)
  local copies, waits for them, and re-layouts  32 us (10%)
  between operations  15 us (5%)
  other arithmetic  13 us (4%)
    all_gather x1, waiting for transfers between devices, body(): lax.all_gather(data, 'param', axis=1, tiled=True)  101 us
    dot_general x4, matrix products, contract(): jnp.einsum('spf,rsf->rpf', kernel, spectrum, precision=lax.Precision.HIGH...  56.8 us
    dot_general x1, matrix products, to_spectrum(): jnp.dot(series.reshape(vectors * sensors, steps), forward, precision=lax....  51.7 us
    psum x1, blocking collectives, body(): squares = lax.psum(jnp.sum(share * share, axis=(1, 2)), 'param')  35.2 us
    unnamed x20, local copies, waits for them, and re-layouts  18.2 us
    dot_general x8, local copies, waits for them, and re-layouts, contract(): jnp.einsum('spf,rsf->rpf', kernel, spectrum, precision=lax.Precision.HIGH...  13.8 us
    all_gather x1, blocking collectives, body(): lax.all_gather(normalized, 'sensor', axis=0, tiled=True)  8.61 us
    reduce_scatter x1, waiting for transfers between devices, body(): lax.psum_scatter(partial_field, 'sensor', scatter_dimension=0, tiled=True)  7.34 us
  transfers between devices with their start and end apart: 2, of which 2 were waited for; matrix products, arithmetic and copies ran while one was open for 5% of the time, Pallas kernels for 0%

commit v1 on v0

--- a/solution.py
+++ b/solution.py
@@ -1,9 +1,18 @@
+import functools
 import math
 
 import jax
 import jax.numpy as jnp
+import numpy as np
 from jax import lax
+from jax.experimental import pallas as pl
+from jax.experimental.pallas import tpu as pltpu
 from jax.sharding import PartitionSpec as P
+
+MESH = pl.DeviceIdType.MESH
+LANES = 128
+GROUP = 8
+CHUNKS = 4
 
 
 def spectral_tables(steps):
@@ -39,7 +48,7 @@
     )
 
 
-def body(data, spectra):
+def general_body(data, spectra):
     steps = data.shape[2]
     freqs = steps + 1
     forward, backward = spectral_tables(steps)
@@ -67,7 +76,400 @@
     return (gradient, rms_all)
 
 
+def split(value):
+    high = value.astype(jnp.bfloat16)
+    return high, (value - high.astype(jnp.float32)).astype(jnp.bfloat16)
+
+
+NT_DIMS = (((1,), (1,)), ((), ()))
+
+
+def product(left, right, dims):
+    dot = functools.partial(lax.dot_general, dimension_numbers=dims, preferred_element_type=jnp.float32)
+    return dot(left[0], right[0]) + (dot(left[0], right[1]) + dot(left[1], right[0]))
+
+
+def kernel(
+    n, lines, vectors, local, steps, points, freqs, padded, wide,
+    data_ref, spectra_ref, table_ref,
+    out_ref, rms_ref,
+    gathered, kbuf, table, even_h, even_l, odd_h, odd_l, spectrum, product_s, partial, pairs, square, squares,
+    load_sem, swap_send, swap_recv, kswap_send, kswap_recv, z_send, z_recv, y_send, y_recv, c_send, c_recv,
+    f_send, f_recv, r_send, r_recv,
+):
+    me = lax.axis_index("param")
+    core = lax.axis_index("sensor")
+    x = lax.rem(me, 2)
+    y = lax.rem(me // 2, 2)
+    z = me // 4
+    plane = 4
+    other_chip = me + 1 - 2 * x
+    y_chip = me + 2 - 4 * y
+    other_core = 1 - core
+    swapped = x != core
+    kept = x == core
+    per = (vectors // 2) // CHUNKS
+
+    table_copy = pltpu.make_async_copy(table_ref, table, load_sem.at[0])
+    table_copy.start()
+    kbuf[:, freqs:] = jnp.zeros((2, padded - freqs) + tuple(kbuf.shape[2:]), jnp.float32)
+
+    barrier = pltpu.get_barrier_semaphore()
+
+    @pl.loop(1, n)
+    def _(step):
+        pl.semaphore_signal(barrier, inc=1, device_id=(lax.rem(me + step, n), core), device_id_type=MESH)
+
+    pl.semaphore_signal(barrier, inc=1, device_id=(me, other_core), device_id_type=MESH)
+    pl.semaphore_signal(barrier, inc=1, device_id=(other_chip, other_core), device_id_type=MESH)
+    pl.semaphore_wait(barrier, n + 1)
+
+    def slot(line, row, column):
+        return line * plane + row * 2 + column
+
+    def block(chunk, position):
+        return gathered.at[pl.ds(chunk * per, per), pl.ds(pl.multiple_of(position * local, local), local), :]
+
+    mine = slot(z, y, core)
+
+    def swap(chunk):
+        return pltpu.make_async_remote_copy(
+            src_ref=data_ref.at[pl.ds(chunk * per, per)],
+            dst_ref=block(chunk, slot(z, y, other_core)),
+            send_sem=swap_send.at[chunk], recv_sem=swap_recv.at[chunk],
+            device_id=(other_chip, other_core), device_id_type=MESH,
+        )
+
+    def keep(chunk):
+        return pltpu.make_async_copy(data_ref.at[pl.ds(chunk * per, per)], block(chunk, mine), swap_recv.at[chunk])
+
+    def kswap(part):
+        return pltpu.make_async_remote_copy(
+            src_ref=spectra_ref.at[part], dst_ref=kbuf.at[part, pl.ds(0, freqs)],
+            send_sem=kswap_send.at[part], recv_sem=kswap_recv.at[part],
+            device_id=(other_chip, other_core), device_id_type=MESH,
+        )
+
+    def kkeep(part):
+        return pltpu.make_async_copy(spectra_ref.at[part], kbuf.at[part, pl.ds(0, freqs)], kswap_recv.at[part])
+
+    @pl.when(swapped)
+    def _():
+        for chunk in range(CHUNKS):
+            swap(chunk).start()
+        for part in range(2):
+            kswap(part).start()
+
+    @pl.when(kept)
+    def _():
+        for chunk in range(CHUNKS):
+            keep(chunk).start()
+        for part in range(2):
+            kkeep(part).start()
+
+    def send(chunk, position, target, send_sem, recv_sem):
+        return pltpu.make_async_remote_copy(
+            src_ref=block(chunk, position), dst_ref=block(chunk, position),
+            send_sem=send_sem, recv_sem=recv_sem, device_id=target, device_id_type=MESH,
+        )
+
+    def line_copy(chunk, step):
+        target = lax.rem(z + step, lines)
+        return send(chunk, mine, (slot(target, y, x), core), z_send.at[chunk, step], z_recv.at[chunk, step])
+
+    def y_copy(chunk, step):
+        return send(
+            chunk, slot(lax.rem(z + lines - step, lines), y, core), (y_chip, core),
+            y_send.at[chunk, step], y_recv.at[chunk, step],
+        )
+
+    def core_copy(chunk, row, step):
+        position = slot(lax.rem(z + lines - step, lines), row, core)
+        index = step + lines * jnp.where(row == y, 0, 1)
+        return send(chunk, position, (me, other_core), c_send.at[chunk, index], c_recv.at[chunk, index])
+
+    def start_lines(chunk):
+        @pl.when(swapped)
+        def _():
+            swap(chunk).wait_recv()
+
+        @pl.when(kept)
+        def _():
+            keep(chunk).wait()
+
+        for step in range(1, lines):
+            line_copy(chunk, step).start()
+        y_copy(chunk, 0).start()
+        core_copy(chunk, y, 0).start()
+
+    def from_lines(chunk):
+        for step in range(1, lines):
+            line_copy(chunk, step).wait_recv()
+            y_copy(chunk, step).start()
+            core_copy(chunk, y, step).start()
+
+    def from_row(chunk):
+        for step in range(lines):
+            y_copy(chunk, step).wait_recv()
+            core_copy(chunk, 1 - y, step).start()
+
+    def from_core(chunk):
+        for step in range(lines):
+            core_copy(chunk, y, step).wait_recv()
+            core_copy(chunk, 1 - y, step).wait_recv()
+
+    def transform(chunk):
+        @pl.loop(0, per)
+        def _(pair):
+            r2 = chunk * per + pair
+            for half, high, low in ((0, even_h, even_l), (1, odd_h, odd_l)):
+                begin = half * (gathered.shape[2] - wide)
+                series = split(gathered[r2, :, begin : begin + wide])
+
+                @pl.loop(0, 2)
+                def _(imag):
+                    rows = pl.ds(pl.multiple_of(imag * padded, 16), padded)
+                    result = product((high[rows, :], low[rows, :]), series, NT_DIMS)
+                    for lane in range(2):
+                        spectrum[lane, pl.ds(imag * vectors + 2 * r2 + half, padded, stride=2 * vectors), :] = result[
+                            :, lane * LANES : (lane + 1) * LANES
+                        ]
+
+    for chunk in range(CHUNKS):
+        start_lines(chunk)
+
+    table_copy.wait()
+    shift = 2 * steps - (gathered.shape[2] - wide) - steps
+    values = table[...]
+    even_h[...], even_l[...] = split(values)
+    odd_h[...], odd_l[...] = split(pltpu.roll(values, shift, 1))
+
+    from_lines(0)
+    for chunk in range(CHUNKS):
+        if chunk + 1 < CHUNKS:
+            from_lines(chunk + 1)
+        from_row(chunk)
+        from_core(chunk)
+        transform(chunk)
+
+    @pl.when(swapped)
+    def _():
+        for part in range(2):
+            kswap(part).wait_recv()
+
+    @pl.when(kept)
+    def _():
+        for part in range(2):
+            kkeep(part).wait()
+
+    rows = GROUP * points
+    columns = GROUP * 2 * vectors
+    row_freq = lax.broadcasted_iota(jnp.int32, (2 * rows, columns), 0) // points % GROUP
+    col_freq = lax.broadcasted_iota(jnp.int32, (2 * rows, columns), 1) // (2 * vectors)
+    own = row_freq == col_freq
+    lane = lax.broadcasted_iota(jnp.int32, (rows, LANES), 1)
+    sign = jnp.where(lane % (2 * vectors) < vectors, 1.0, -1.0)
+    row = lax.broadcasted_iota(jnp.int32, (rows, LANES), 0) // points
+
+    @pl.loop(0, padded // GROUP)
+    def _(group):
+        begin = pl.multiple_of(group * columns, columns)
+        right = split(
+            jnp.concatenate([spectrum[0, pl.ds(begin, columns), :], spectrum[1, pl.ds(begin, columns), :]], axis=1)
+        )
+        left = jnp.concatenate(
+            [kbuf[part, pl.ds(group * GROUP, GROUP)].reshape(rows, kbuf.shape[3]) for part in range(2)], axis=0
+        )
+        found = jnp.where(own, product(split(left), right, NT_DIMS), 0.0)
+        width = columns
+        while width > LANES:
+            width //= 2
+            found = found[:, :width] + found[:, width:]
+        hop = LANES // 2
+        while hop >= 2 * vectors:
+            found = found + pltpu.roll(found, hop, 1)
+            hop //= 2
+        value = found[:rows] + sign * pltpu.roll(found[rows:], vectors, 1)
+        freq = row + group * GROUP
+        weight = jnp.where((freq == 0) | (freq == freqs - 1), 0.5 / steps, 1.0 / steps)
+        product_s[pl.ds(pl.multiple_of(group * rows, rows), rows), :] = value * weight
+
+    lanes = lax.broadcasted_iota(jnp.int32, (padded, LANES), 1) // (2 * vectors)
+    merged = jnp.zeros((padded, LANES), jnp.float32)
+    for point in range(points):
+        merged = jnp.where(lanes == point, product_s[pl.ds(point, padded, stride=points), :], merged)
+    turned = split(merged.T)
+    plain = (((1,), (0,)), ((), ()))
+    real = product(turned, (even_h[:padded, :], even_l[:padded, :]), plain)
+    imag = product(turned, (even_h[padded:, :], even_l[padded:, :]), plain)
+    for point in range(points):
+        first = point * 2 * vectors
+        field = real[first : first + vectors] + imag[first + vectors : first + 2 * vectors]
+        partial[point * vectors : (point + 1) * vectors, :] = field
+
+    def field_copy(target):
+        return pltpu.make_async_remote_copy(
+            src_ref=partial, dst_ref=pairs.at[x], send_sem=f_send.at[target], recv_sem=f_recv.at[x],
+            device_id=(me - x + core, target), device_id_type=MESH,
+        )
+
+    def field_arrival(group):
+        return pltpu.make_async_remote_copy(
+            src_ref=partial, dst_ref=pairs.at[group], send_sem=f_send.at[0], recv_sem=f_recv.at[group],
+            device_id=(other_chip, other_core), device_id_type=MESH,
+        )
+
+    @pl.when(swapped)
+    def _():
+        field_copy(0).start()
+        field_copy(1).start()
+
+    @pl.when(kept)
+    def _():
+        field_copy(other_core).start()
+        pairs[x] = partial[...]
+
+    field_arrival(1 - x).wait_recv()
+
+    @pl.when(swapped)
+    def _():
+        field_arrival(x).wait_recv()
+
+    total = pairs[0] + pairs[1]
+    energy = total * total
+    folded = energy[:vectors]
+    for point in range(1, points):
+        folded = folded + energy[point * vectors : (point + 1) * vectors]
+    summed = jnp.broadcast_to(jnp.sum(folded, axis=1, keepdims=True), (vectors, LANES))
+    square[...] = summed
+    squares[me] = summed
+
+    def square_copy(step):
+        return pltpu.make_async_remote_copy(
+            src_ref=square, dst_ref=squares.at[me], send_sem=r_send.at[step], recv_sem=r_recv.at[step],
+            device_id=(lax.rem(me + step, n), core), device_id_type=MESH,
+        )
+
+    def square_arrival(step):
+        return pltpu.make_async_remote_copy(
+            src_ref=square, dst_ref=squares.at[lax.rem(me + n - step, n)],
+            send_sem=r_send.at[step], recv_sem=r_recv.at[step],
+            device_id=(lax.rem(me + step, n), core), device_id_type=MESH,
+        )
+
+    @pl.loop(1, n)
+    def _(step):
+        square_copy(step).start()
+
+    for chunk in range(CHUNKS):
+        for step in range(1, lines):
+            line_copy(chunk, step).wait_send()
+        for step in range(lines):
+            y_copy(chunk, step).wait_send()
+            core_copy(chunk, y, step).wait_send()
+            core_copy(chunk, 1 - y, step).wait_send()
+
+    @pl.when(swapped)
+    def _():
+        for chunk in range(CHUNKS):
+            swap(chunk).wait_send()
+        for part in range(2):
+            kswap(part).wait_send()
+        field_copy(0).wait_send()
+        field_copy(1).wait_send()
+
+    @pl.when(kept)
+    def _():
+        field_copy(other_core).wait_send()
+
+    @pl.loop(1, n)
+    def _(step):
+        square_arrival(step).wait()
+
+    energy_all = squares[0]
+    for device in range(1, n):
+        energy_all = energy_all + squares[device]
+    scale = jnp.sqrt(energy_all / (points * n * steps) + 1e-06)
+    rms_ref[...] = scale
+    inverse = scale[:, :1]
+    for point in range(points):
+        out_ref[point] = total[point * vectors : (point + 1) * vectors, :steps] / inverse
+
+
+def paired_body(data, spectra):
+    n = lax.axis_size("param")
+    vectors, local, steps = data.shape
+    sensors, points, freqs = spectra.shape[1:]
+    wide = -(-steps // LANES) * LANES
+    packed = -(-2 * steps // LANES) * LANES
+    padded = -(-freqs // 16) * 16
+    times = np.arange(steps)[None, :]
+    bins = np.arange(freqs)[:, None]
+    phase = np.pi / steps * (times * bins % (2 * steps))
+    host = np.zeros((2, padded, wide), np.float32)
+    host[0, :freqs, :steps] = np.cos(phase)
+    host[1, :freqs, :steps] = -np.sin(phase)
+    table = jnp.asarray(host.reshape(2 * padded, wide))
+    lines = n // 4
+
+    halves = data.reshape(vectors // 2, 2, local, steps)
+    series = jnp.concatenate([halves[:, 0], halves[:, 1]], axis=-1)
+    series = jnp.pad(series, ((0, 0), (0, 0), (0, packed - 2 * steps)))
+    turned = jnp.transpose(spectra, (0, 3, 2, 1))
+
+    hbm = pl.BlockSpec(memory_space=pl.ANY)
+    vmem = pl.BlockSpec(memory_space=pltpu.VMEM)
+    dma = pltpu.SemaphoreType.DMA
+    f32, bf16 = jnp.float32, jnp.bfloat16
+    fields, scale = pl.pallas_call(
+        functools.partial(kernel, n, lines, vectors, local, steps, points, freqs, padded, wide),
+        out_shape=(
+            jax.ShapeDtypeStruct((points, vectors, steps), f32),
+            jax.ShapeDtypeStruct((vectors, LANES), f32),
+        ),
+        in_specs=[hbm, hbm, hbm],
+        out_specs=(vmem, vmem),
+        scratch_shapes=[
+            pltpu.VMEM((vectors // 2, sensors, packed), f32),
+            pltpu.VMEM((2, padded, points, sensors), f32),
+            pltpu.VMEM((2 * padded, wide), f32),
+            pltpu.VMEM((2 * padded, wide), bf16),
+            pltpu.VMEM((2 * padded, wide), bf16),
+            pltpu.VMEM((2 * padded, wide), bf16),
+            pltpu.VMEM((2 * padded, wide), bf16),
+            pltpu.VMEM((2, padded * 2 * vectors, LANES), f32),
+            pltpu.VMEM((padded * points, LANES), f32),
+            pltpu.VMEM((points * vectors, wide), f32),
+            pltpu.VMEM((2, points * vectors, wide), f32),
+            pltpu.VMEM((vectors, LANES), f32),
+            pltpu.VMEM((n, vectors, LANES), f32),
+            dma((1,)),
+            dma((CHUNKS,)), dma((CHUNKS,)),
+            dma((2,)), dma((2,)),
+            dma((CHUNKS, lines)), dma((CHUNKS, lines)),
+            dma((CHUNKS, lines)), dma((CHUNKS, lines)),
+            dma((CHUNKS, 2 * lines)), dma((CHUNKS, 2 * lines)),
+            dma((2,)), dma((2,)),
+            dma((n,)), dma((n,)),
+        ],
+        compiler_params=pltpu.CompilerParams(
+            collective_id=0, has_side_effects=True, vmem_limit_bytes=60 * 1024 * 1024
+        ),
+    )(series, turned, table)
+    return (jnp.transpose(fields, (1, 0, 2)), scale[:, 0])
+
+
 def solution(mesh):
     in_specs = (P(None, ("sensor", "param"), None), P(None, "sensor", "param", None))
     out_specs = (P(None, "param", None), P())
+    n = mesh.shape["param"]
+    pair = mesh.shape["sensor"] == 2 and n == 16
+
+    def body(data, spectra):
+        vectors, local, _ = data.shape
+        sensors, points = spectra.shape[1:3]
+        fits = local % 8 == 0 and sensors == 2 * LANES and vectors % (2 * CHUNKS) == 0
+        fits = fits and vectors % 8 == 0 and points * 2 * vectors == LANES
+        return (paired_body if pair and fits else general_body)(data, spectra)
+
     return jax.shard_map(body, mesh=mesh, in_specs=in_specs, out_specs=out_specs, check_vma=False)

time: 330 us -> 122 us (0.37); the launches traced: 326 us -> 122 us
  Pallas kernels: 0 us -> 116 us
  matrix products: 111 us -> 0 us
  waiting for transfers between devices: 109 us -> 0 us
  blocking collectives: 46.7 us -> 0 us
  local copies, waits for them, and re-layouts: 32 us -> 4.04 us
  between operations: 15 us -> 0.65 us
  other arithmetic: 13 us -> 0.91 us
    pallas_call x0 -> x1, Pallas kernels: none -> 116 us  [paired_body(): pl.pallas_call(functools.partial(kernel, n, lines, vectors, local, steps,...]
    dot_general x6 -> x0, matrix products: 111 us -> none  [the longest x4 56.8 us: contract(): jnp.einsum('spf,rsf->rpf', kernel, spectrum, precision=lax.Precision.HIGH...]
    all_gather x1 -> x0, waiting for transfers between devices: 101 us -> none  [body(): lax.all_gather(data, 'param', axis=1, tiled=True)]
    psum x1 -> x0, blocking collectives: 35.2 us -> none  [body(): squares = lax.psum(jnp.sum(share * share, axis=(1, 2)), 'param')]
    unnamed x20 -> x1, local copies, waits for them, and re-layouts: 18.2 us -> 1.65 us
    dot_general x8 -> x0, local copies, waits for them, and re-layouts: 13.8 us -> none  [contract(): jnp.einsum('spf,rsf->rpf', kernel, spectrum, precision=lax.Precision.HIGH...]
    all_gather x1 -> x0, blocking collectives: 8.61 us -> none  [body(): lax.all_gather(normalized, 'sensor', axis=0, tiled=True)]
    reduce_scatter x1 -> x0, waiting for transfers between devices: 7.34 us -> none  [body(): lax.psum_scatter(partial_field, 'sensor', scatter_dimension=0, tiled=True)]
  transfers between devices with their start and end apart: 2 -> 0, of which waited for: 2 -> 0; matrix products, arithmetic and copies ran while one was open for 5% -> 0% of each run, Pallas kernels for 0% -> 0%
where the time goes in v1:
time: 122 us
  Pallas kernels  116 us (95%)
  local copies, waits for them, and re-layouts  4.04 us (3%)
    pallas_call x1, Pallas kernels, paired_body(): pl.pallas_call(functools.partial(kernel, n, lines, vectors, local, steps,...  116 us

profile of v1, /device:TPU:1, one launch (start us, length us, event | category | flops | bytes accessed | tf_op | source)
XLA Modules:
  0.0 122.0 jit_solution(1484550451870396659)
XLA Ops:
  0.6 1.1 slice_bitcast_fusion.1
  1.7 0.9 select_maximum_fusion.data_ref
  2.6 116.4 %shard_map.50 = (f32[4,16,420]{2,1,0:T(8,128)}, f32[16,128]{1,0:T(8,128)}) custom-call(f32[8,16,896]{2,1,0:T(8,128)} %select_maximum_fusion.data_ref, f32[2,421,4,256]{3,2,1,0:T(4,128)} %bitcast.11, f32[864,512]{1,0:T(8,128)} %constant.5.clone.table_ref), custom_call_target="tpu_custom_call" | custom-call | tf_op jit(solution)/shard_map/pallas_call | solution.py:424
  119.0 1.6 %copy.8 = f32[16,4,420]{2,1,0:T(4,128)} copy(f32[16,4,420]{2,0,1:T(8,128)} %bitcast.13) | data formatting | bytes 215040
  120.7 1.3 %slice_reduce_fusion = f32[16]{0:T(128)} fusion(f32[16,128]{1,0:T(8,128)} %get-tuple-element.5), kind=kLoop, calls=%fused_computation.4 | loop fusion | bytes 128 | tf_op jit(solution)/shard_map/slice | solution.py:459

commit v2 on v1

--- a/solution.py
+++ b/solution.py
@@ -12,7 +12,7 @@
 MESH = pl.DeviceIdType.MESH
 LANES = 128
 GROUP = 8
-CHUNKS = 4
+CHUNKS = 8
 
 
 def spectral_tables(steps):
@@ -86,7 +86,9 @@
 
 def product(left, right, dims):
     dot = functools.partial(lax.dot_general, dimension_numbers=dims, preferred_element_type=jnp.float32)
-    return dot(left[0], right[0]) + (dot(left[0], right[1]) + dot(left[1], right[0]))
+    size = left[0].shape[0]
+    both = dot(jnp.concatenate(left, axis=0), right[0])
+    return both[:size] + (both[size:] + dot(left[0], right[1]))
 
 
 def kernel(
@@ -140,6 +142,13 @@
             device_id=(other_chip, other_core), device_id_type=MESH,
         )
 
+    def swap_arrival(chunk):
+        return pltpu.make_async_remote_copy(
+            src_ref=data_ref.at[pl.ds(chunk * per, per)], dst_ref=block(chunk, mine),
+            send_sem=swap_send.at[chunk], recv_sem=swap_recv.at[chunk],
+            device_id=(other_chip, other_core), device_id_type=MESH,
+        )
+
     def keep(chunk):
         return pltpu.make_async_copy(data_ref.at[pl.ds(chunk * per, per)], block(chunk, mine), swap_recv.at[chunk])
 
@@ -173,50 +182,91 @@
             send_sem=send_sem, recv_sem=recv_sem, device_id=target, device_id_type=MESH,
         )
 
-    def line_copy(chunk, step):
-        target = lax.rem(z + step, lines)
-        return send(chunk, mine, (slot(target, y, x), core), z_send.at[chunk, step], z_recv.at[chunk, step])
-
-    def y_copy(chunk, step):
+    def line_copy(chunk, step, way):
+        source = jnp.clip(z - way * step, 0, lines - 1)
+        target = jnp.clip(z + way, 0, lines - 1)
+        index = step if way > 0 else lines + step
         return send(
-            chunk, slot(lax.rem(z + lines - step, lines), y, core), (y_chip, core),
-            y_send.at[chunk, step], y_recv.at[chunk, step],
-        )
-
-    def core_copy(chunk, row, step):
-        position = slot(lax.rem(z + lines - step, lines), row, core)
-        index = step + lines * jnp.where(row == y, 0, 1)
-        return send(chunk, position, (me, other_core), c_send.at[chunk, index], c_recv.at[chunk, index])
+            chunk, slot(source, y, core), (slot(target, y, x), core), z_send.at[chunk, index], z_recv.at[chunk, index]
+        )
+
+    def line_arrival(chunk, step, way):
+        source = jnp.clip(z - way * (step + 1), 0, lines - 1)
+        target = jnp.clip(z + way, 0, lines - 1)
+        index = step if way > 0 else lines + step
+        return source, send(
+            chunk, slot(source, y, core), (slot(target, y, x), core), z_send.at[chunk, index], z_recv.at[chunk, index]
+        )
+
+    def sends(step, way):
+        inside = z + 1 < lines if way > 0 else z > 0
+        begun = z >= step if way > 0 else z + step < lines
+        return jnp.logical_and(inside, begun)
+
+    def receives(step, way):
+        return z >= step + 1 if way > 0 else z + step + 1 < lines
+
+    def y_copy(chunk, line):
+        return send(chunk, slot(line, y, core), (y_chip, core), y_send.at[chunk, line], y_recv.at[chunk, line])
+
+    def y_arrival(chunk, line):
+        return send(chunk, slot(line, 1 - y, core), (y_chip, core), y_send.at[chunk, line], y_recv.at[chunk, line])
+
+    def core_copy(chunk, row, line):
+        index = row * lines + line
+        return send(chunk, slot(line, row, core), (me, other_core), c_send.at[chunk, index], c_recv.at[chunk, index])
+
+    def core_arrival(chunk, row, line):
+        index = row * lines + line
+        return send(
+            chunk, slot(line, row, other_core), (me, other_core), c_send.at[chunk, index], c_recv.at[chunk, index]
+        )
 
     def start_lines(chunk):
         @pl.when(swapped)
         def _():
-            swap(chunk).wait_recv()
+            swap_arrival(chunk).wait_recv()
 
         @pl.when(kept)
         def _():
             keep(chunk).wait()
 
-        for step in range(1, lines):
-            line_copy(chunk, step).start()
-        y_copy(chunk, 0).start()
-        core_copy(chunk, y, 0).start()
+        for way in (1, -1):
+
+            @pl.when(sends(0, way))
+            def _():
+                line_copy(chunk, 0, way).start()
+
+        y_copy(chunk, z).start()
+        core_copy(chunk, y, z).start()
 
     def from_lines(chunk):
-        for step in range(1, lines):
-            line_copy(chunk, step).wait_recv()
-            y_copy(chunk, step).start()
-            core_copy(chunk, y, step).start()
+        for step in range(lines - 1):
+            for way in (1, -1):
+
+                @pl.when(receives(step, way))
+                def _():
+                    source, arrival = line_arrival(chunk, step, way)
+                    arrival.wait_recv()
+                    if step + 1 < lines - 1:
+
+                        @pl.when(sends(step + 1, way))
+                        def _():
+                            line_copy(chunk, step + 1, way).start()
+
+                    y_copy(chunk, source).start()
+                    core_copy(chunk, y, source).start()
 
     def from_row(chunk):
         for step in range(lines):
-            y_copy(chunk, step).wait_recv()
-            core_copy(chunk, 1 - y, step).start()
+            line = lax.rem(z + step, lines)
+            y_arrival(chunk, line).wait_recv()
+            core_copy(chunk, 1 - y, line).start()
 
     def from_core(chunk):
-        for step in range(lines):
-            core_copy(chunk, y, step).wait_recv()
-            core_copy(chunk, 1 - y, step).wait_recv()
+        for line in range(lines):
+            for row in range(2):
+                core_arrival(chunk, row, line).wait_recv()
 
     def transform(chunk):
         @pl.loop(0, per)
@@ -235,8 +285,7 @@
                             :, lane * LANES : (lane + 1) * LANES
                         ]
 
-    for chunk in range(CHUNKS):
-        start_lines(chunk)
+    pl.loop(0, CHUNKS)(start_lines)
 
     table_copy.wait()
     shift = 2 * steps - (gathered.shape[2] - wide) - steps
@@ -245,9 +294,13 @@
     odd_h[...], odd_l[...] = split(pltpu.roll(values, shift, 1))
 
     from_lines(0)
-    for chunk in range(CHUNKS):
-        if chunk + 1 < CHUNKS:
+
+    @pl.loop(0, CHUNKS)
+    def _(chunk):
+        @pl.when(chunk + 1 < CHUNKS)
+        def _():
             from_lines(chunk + 1)
+
         from_row(chunk)
         from_core(chunk)
         transform(chunk)
@@ -271,7 +324,7 @@
     sign = jnp.where(lane % (2 * vectors) < vectors, 1.0, -1.0)
     row = lax.broadcasted_iota(jnp.int32, (rows, LANES), 0) // points
 
-    @pl.loop(0, padded // GROUP)
+    @pl.loop(0, padded // GROUP, unroll=3)
     def _(group):
         begin = pl.multiple_of(group * columns, columns)
         right = split(
@@ -361,13 +414,19 @@
     def _(step):
         square_copy(step).start()
 
-    for chunk in range(CHUNKS):
-        for step in range(1, lines):
-            line_copy(chunk, step).wait_send()
-        for step in range(lines):
-            y_copy(chunk, step).wait_send()
-            core_copy(chunk, y, step).wait_send()
-            core_copy(chunk, 1 - y, step).wait_send()
+    @pl.loop(0, CHUNKS)
+    def _(chunk):
+        for step in range(lines - 1):
+            for way in (1, -1):
+
+                @pl.when(sends(step, way))
+                def _():
+                    line_copy(chunk, step, way).wait_send()
+
+        for line in range(lines):
+            y_copy(chunk, line).wait_send()
+            for row in range(2):
+                core_copy(chunk, row, line).wait_send()
 
     @pl.when(swapped)
     def _():
@@ -446,7 +505,7 @@
             dma((1,)),
             dma((CHUNKS,)), dma((CHUNKS,)),
             dma((2,)), dma((2,)),
-            dma((CHUNKS, lines)), dma((CHUNKS, lines)),
+            dma((CHUNKS, 2 * lines)), dma((CHUNKS, 2 * lines)),
             dma((CHUNKS, lines)), dma((CHUNKS, lines)),
             dma((CHUNKS, 2 * lines)), dma((CHUNKS, 2 * lines)),
             dma((2,)), dma((2,)),

time: 122 us -> 117 us (0.959)
  Pallas kernels: 116 us -> 111 us
    pallas_call x1, Pallas kernels: 116 us -> 111 us  [paired_body(): pl.pallas_call(functools.partial(kernel, n, lines, vectors, local, steps,...]
where the time goes in v2:
time: 117 us
  Pallas kernels  111 us (95%)
  local copies, waits for them, and re-layouts  4.04 us (3%)
    pallas_call x1, Pallas kernels, paired_body(): pl.pallas_call(functools.partial(kernel, n, lines, vectors, local, steps,...  111 us

profile of v2, /device:TPU:1, one launch (start us, length us, event | category | flops | bytes accessed | tf_op | source)
XLA Modules:
  0.0 117.1 jit_solution(12282878912844366576)
XLA Ops:
  0.6 1.1 slice_bitcast_fusion.1
  1.7 0.9 select_maximum_fusion.data_ref
  2.6 111.5 %shard_map.50 = (f32[4,16,420]{2,1,0:T(8,128)}, f32[16,128]{1,0:T(8,128)}) custom-call(f32[8,16,896]{2,1,0:T(8,128)} %select_maximum_fusion.data_ref, f32[2,421,4,256]{3,2,1,0:T(4,128)} %bitcast.11, f32[864,512]{1,0:T(8,128)} %constant.5.clone.table_ref), custom_call_target="tpu_custom_call" | custom-call | tf_op jit(solution)/shard_map/pallas_call | solution.py:483
  114.1 1.6 %copy.8 = f32[16,4,420]{2,1,0:T(4,128)} copy(f32[16,4,420]{2,0,1:T(8,128)} %bitcast.13) | data formatting | bytes 215040
  115.7 1.3 %slice_reduce_fusion = f32[16]{0:T(128)} fusion(f32[16,128]{1,0:T(8,128)} %get-tuple-element.5), kind=kLoop, calls=%fused_computation.4 | loop fusion | bytes 128 | tf_op jit(solution)/shard_map/slice | solution.py:518

commit v3 on v2

--- a/solution.py
+++ b/solution.py
@@ -240,22 +240,21 @@
         y_copy(chunk, z).start()
         core_copy(chunk, y, z).start()
 
-    def from_lines(chunk):
-        for step in range(lines - 1):
-            for way in (1, -1):
-
-                @pl.when(receives(step, way))
-                def _():
-                    source, arrival = line_arrival(chunk, step, way)
-                    arrival.wait_recv()
-                    if step + 1 < lines - 1:
-
-                        @pl.when(sends(step + 1, way))
-                        def _():
-                            line_copy(chunk, step + 1, way).start()
-
-                    y_copy(chunk, source).start()
-                    core_copy(chunk, y, source).start()
+    def from_lines(chunk, step):
+        for way in (1, -1):
+
+            @pl.when(receives(step, way))
+            def _():
+                source, arrival = line_arrival(chunk, step, way)
+                arrival.wait_recv()
+                if step + 1 < lines - 1:
+
+                    @pl.when(sends(step + 1, way))
+                    def _():
+                        line_copy(chunk, step + 1, way).start()
+
+                y_copy(chunk, source).start()
+                core_copy(chunk, y, source).start()
 
     def from_row(chunk):
         for step in range(lines):
@@ -293,17 +292,20 @@
     even_h[...], even_l[...] = split(values)
     odd_h[...], odd_l[...] = split(pltpu.roll(values, shift, 1))
 
-    from_lines(0)
-
-    @pl.loop(0, CHUNKS)
-    def _(chunk):
-        @pl.when(chunk + 1 < CHUNKS)
-        def _():
-            from_lines(chunk + 1)
-
-        from_row(chunk)
+    def finish(chunk):
         from_core(chunk)
         transform(chunk)
+
+    stages = [functools.partial(from_lines, step=step) for step in range(lines - 1)] + [from_row, finish]
+
+    @pl.loop(0, CHUNKS + len(stages) - 1)
+    def _(turn):
+        for age, stage in enumerate(stages):
+            chunk = turn - age
+
+            @pl.when(jnp.logical_and(chunk >= 0, chunk < CHUNKS))
+            def _():
+                stage(chunk)
 
     @pl.when(swapped)
     def _():

time: 117 us -> 95.4 us (0.82)
  Pallas kernels: 111 us -> 89.6 us
    pallas_call x1, Pallas kernels: 111 us -> 89.6 us  [paired_body(): pl.pallas_call(functools.partial(kernel, n, lines, vectors, local, steps,...]
where the time goes in v3:
time: 95.4 us; the launch traced here: 95.2 us
  Pallas kernels  89.6 us (94%)
  local copies, waits for them, and re-layouts  4.04 us (4%)
    pallas_call x1, Pallas kernels, paired_body(): pl.pallas_call(functools.partial(kernel, n, lines, vectors, local, steps,...  89.6 us

profile of v3, /device:TPU:1, one launch (start us, length us, event | category | flops | bytes accessed | tf_op | source)
XLA Modules:
  0.0 95.2 jit_solution(3576791516763925318)
XLA Ops:
  0.6 1.1 %slice_bitcast_fusion.1 = (f32[8,16,420]{2,1,0:T(8,128)S(1)}, f32[8,16,420]{2,1,0:T(8,128)S(1)}) fusion(f32[8,2,16,420]{3,2,1,0:T(8,128)} %bitcast.12), kind=kLoop, calls=%fused_computation.3 | loop fusion | bytes 860160 | tf_op jit(solution)/shard_map/squeeze | solution.py:477
  1.7 0.9 select_maximum_fusion.data_ref
  2.6 89.6 %shard_map.50 = (f32[4,16,420]{2,1,0:T(8,128)}, f32[16,128]{1,0:T(8,128)}) custom-call(f32[8,16,896]{2,1,0:T(8,128)} %select_maximum_fusion.data_ref, f32[2,421,4,256]{3,2,1,0:T(4,128)} %bitcast.11, f32[864,512]{1,0:T(8,128)} %constant.5.clone.table_ref), custom_call_target="tpu_custom_call" | custom-call | tf_op jit(solution)/shard_map/pallas_call | solution.py:485
  92.2 1.6 %copy.8 = f32[16,4,420]{2,1,0:T(4,128)} copy(f32[16,4,420]{2,0,1:T(8,128)} %bitcast.13) | data formatting | bytes 215040
  93.9 1.3 %slice_reduce_fusion = f32[16]{0:T(128)} fusion(f32[16,128]{1,0:T(8,128)} %get-tuple-element.5), kind=kLoop, calls=%fused_computation.4 | loop fusion | bytes 128 | tf_op jit(solution)/shard_map/slice | solution.py:520
